TPU v7x, 32 devices: a whole 2x2x4 slice. The times are simulated.
32 devices in a mesh: doc: 4 (over y, x), ctx: 8 (over z, core).
Axes of the slice: x: 2, y: 2, z: 4, core: 2. Of those that a mesh axis runs over, the one named last changes fastest.
Arguments:
- summary_cache: bfloat16 [8, 16, 512, 2048], P(None, 'doc', None, 'ctx'), may hold values from -4 to 4
- queries: bfloat16 [4, 2048, 4096], P('doc', 'ctx'), may hold values from -100 to 100
- section_counts: int32 [16], replicated, may hold values from 1 to 2
- summary_blocks: int32 [16, 2], replicated, may hold values from 1 to 2
Outputs:
- attended: bfloat16 [4, 2048, 4096], P('doc', 'ctx')
- relayed: bfloat16 [8, 4, 2048, 2048], P(None, 'doc', 'ctx')
All inputs are finite; a program needn't handle non-finite values.
Results may differ from a plain program's by a relative error of at most 0.0045.
Values may be sent and summed in bfloat16 or wider, within the bound.
A program may use at most 192 MiB of HBM per device.

v0:
```python
import functools
import math

import jax
import jax.numpy as jnp
from jax import lax
from jax.experimental import pallas as pl
from jax.experimental.pallas import tpu as pltpu
from jax.sharding import PartitionSpec as P

QH = 32
KVH = 8
HD = 128
BLOCK = 128
SECTIONS = 2
GROUP = 4
SUMLEN = 256
PARTS = 4


NEGATIVE = -1e30


MESH = pl.DeviceIdType.MESH


def kernel(
    rows,
    ctx,
    cache,
    queries,
    counts,
    blocks,
    attended,
    relayed,
    kv,
    mid,
    stage,
    fwd,
    q_vmem,
    out_vmem,
    bias,
    s1,
    r1_first,
    r1,
    up_sem,
    down_sem,
    side_sem,
    kv_sem,
    s2,
    r2,
    local_sem,
    stage_sem,
    hello,
    fwd_sem,
    s3,
):
    layers, _, slots, feat = cache.shape
    own = queries.shape[0]
    chips = ctx // 2
    parts = kv_sem.shape[2]
    size = slots // parts
    me = lax.axis_index("doc")
    c = lax.axis_index("ctx")
    z = c // 2
    core = c % 2
    binary = rows & (rows - 1) == 0

    def partner(k):
        if not binary:
            return (me + k) % rows
        row, bit = me, 1
        while bit < rows:
            if k & bit:
                row = row + bit * (1 - 2 * ((me // bit) % 2))
            bit *= 2
        return row

    def steps_to(k):
        return bin(k).count("1") if binary else 1

    near = [k for k in range(1, rows) if steps_to(k) == 1]
    rounds = max([steps_to(k) - 1 for k in range(1, rows)])

    def seen(chip):
        return ((2 * chip + 2) * own + slots - 1) // slots

    def greet_rows(sem):
        for k in near:
            pl.semaphore_signal(sem, inc=1, device_id=(partner(k), c), device_id_type=MESH)

    sides = jnp.where(z > 0, 1, 0) + jnp.where(z < chips - 1, 1, 0)
    barrier = pltpu.get_barrier_semaphore()
    for up in (1, -1):

        @pl.when((z + up >= 0) & (z + up < chips))
        def _():
            for other in (core, 1 - core):
                pl.semaphore_signal(barrier, inc=1, device_id=(me, 2 * (z + up) + other), device_id_type=MESH)

    greet_rows(barrier)
    pl.semaphore_signal(barrier, inc=1, device_id=(me, c + 1 - 2 * core), device_id_type=MESH)

    own_kv = pltpu.make_async_copy(
        cache.at[0, me], kv.at[c, pl.ds(pl.multiple_of(me * slots, slots), slots)], local_sem.at[0]
    )
    own_kv.start()

    def staged(k):
        return pltpu.make_async_copy(cache.at[0, partner(k)], stage.at[k - 1], stage_sem.at[k - 1])

    for k in range(1, rows):
        staged(k).start()
    q_copy = pltpu.make_async_copy(queries, q_vmem, local_sem.at[1])
    own_mid = pltpu.make_async_copy(
        cache.at[pl.ds(1, layers - 1), me],
        mid.at[:, pl.ds(pl.multiple_of(me * slots, slots), slots)],
        local_sem.at[2],
    )
    pl.semaphore_wait(barrier, 2 * sides + len(near) + 1)

    def doc(slice_index, j):
        return kv.at[slice_index, pl.ds(pl.multiple_of(j * slots, slots), slots)]

    def part(slice_index, j, h):
        return kv.at[slice_index, pl.ds(pl.multiple_of(j * slots + h * size, size), size)]

    def first_copy(k, j_to, j_from, h):
        return pltpu.make_async_remote_copy(
            src_ref=stage.at[k - 1, pl.ds(h * size, size)],
            dst_ref=part(c, j_from, h),
            send_sem=s1,
            recv_sem=r1_first.at[j_from, h],
            device_id=(j_to, c),
            device_id_type=MESH,
        )

    def row_copy(l, j_to):
        return pltpu.make_async_remote_copy(
            src_ref=cache.at[l, j_to],
            dst_ref=mid.at[l - 1, pl.ds(pl.multiple_of(me * slots, slots), slots)],
            send_sem=s1,
            recv_sem=r1.at[l],
            device_id=(j_to, c),
            device_id_type=MESH,
        )

    def kv_part(slice_index, j, h, sems, target):
        return pltpu.make_async_remote_copy(
            src_ref=part(slice_index, j, h),
            dst_ref=part(slice_index, j, h),
            send_sem=sems.at[slice_index // 2, j],
            recv_sem=kv_sem.at[slice_index, j, h],
            device_id=(me, target),
            device_id_type=MESH,
        )

    def kv_doc(slice_index, j, sems, target):
        return pltpu.make_async_remote_copy(
            src_ref=doc(slice_index, j),
            dst_ref=doc(slice_index, j),
            send_sem=sems.at[slice_index // 2, j],
            recv_sem=kv_sem.at[slice_index, j, 0],
            device_id=(me, target),
            device_id_type=MESH,
        )

    def pass_up(slice_index, j, h):
        @pl.when(z < chips - 1)
        def _():
            kv_part(slice_index, j, h, up_sem, c + 2).start()

    def pass_down(slice_index, j, h):
        @pl.when((z > 0) & (j < seen(z - 1)))
        def _():
            kv_part(slice_index, j, h, down_sem, c - 2).start()

    def pass_side(slice_index, j):
        @pl.when(j < seen(z))
        def _():
            kv_doc(slice_index, j, side_sem, c + 1 - 2 * core).start()

    own_kv.wait()
    for h in range(parts):
        pass_up(c, me, h)
    for k in near:
        staged(k).wait()
    for h in range(parts):
        for k in near:
            first_copy(k, partner(k), me, h).start()
    for h in range(parts):
        pass_down(c, me, h)
    pass_side(c, me)
    own_mid.start()
    q_copy.start()

    for r in range(rounds):
        greet_rows(hello.at[r])
        pl.semaphore_wait(hello.at[r], len(near))
        for k in range(1, rows):
            if steps_to(k) == r + 2:
                staged(k).wait()
                for h in range(parts):
                    first_copy(k, partner(k), me, h).start()

    def from_row(ks):
        for h in range(parts):
            for k in ks:
                j = partner(k)
                first_copy(k, me, j, h).wait_recv()
                pass_up(c, j, h)
                pass_down(c, j, h)
                if h == parts - 1:
                    pass_side(c, j)

    def from_below(step, ks):
        @pl.when(z >= step)
        def _():
            for k in ks:
                j = partner(k)
                for h in range(parts):
                    kv_part(c - 2 * step, j, h, up_sem, c).wait_recv()
                    pass_up(c - 2 * step, j, h)
                pass_side(c - 2 * step, j)

    def from_above(step, ks):
        @pl.when(z + step < chips)
        def _():
            for k in ks:
                j = partner(k)

                @pl.when(j < seen(z))
                def _():
                    for h in range(parts):
                        kv_part(c + 2 * step, j, h, down_sem, c).wait_recv()
                        pass_down(c + 2 * step, j, h)
                    pass_side(c + 2 * step, j)

    both = 2 * own
    half = chips // 2

    def waiting(at, l, s, t):
        ups = at * (chips - 1 - at)
        slot = jnp.where(s < at, s * (chips - 1 - at) + t - at - 1, ups + (s - at - 1) * at + t)
        return fwd.at[l - 1, slot], fwd_sem.at[l - 1, slot]

    def columns(s):
        return pl.ds(pl.multiple_of((2 * s + core) * feat, feat), feat)

    def hop(l, s, m, up, source, sent):
        if m > 1:
            there, arrived = waiting(z + up, l, s, z + up * m)
            pltpu.make_async_remote_copy(
                src_ref=source(0, both),
                dst_ref=there,
                send_sem=sent,
                recv_sem=arrived,
                device_id=(me, c + 2 * up),
                device_id_type=MESH,
            ).start()
        else:
            for other in (core, 1 - core):
                pltpu.make_async_remote_copy(
                    src_ref=source(other * own, own),
                    dst_ref=relayed.at[l, :, columns(s)],
                    send_sem=sent,
                    recv_sem=r2,
                    device_id=(me, 2 * (z + up) + other),
                    device_id_type=MESH,
                ).start()

    def layer_step(l):
        arrived = mid.at[l - 1, pl.ds(0, (rows - 1) * slots)]
        pltpu.make_async_copy(arrived, arrived, r1.at[l]).wait()

        def block(at, length):
            return mid.at[l - 1, pl.ds(pl.multiple_of(at, own), length)]

        for m in range(chips - 1, 0, -1):
            for up in (1, -1):

                @pl.when((z + up * m >= 0) & (z + up * m < chips))
                def _():
                    hop(l, z, m, up, lambda at, length: block((z + up * m) * both + at, length), s2)

        pltpu.make_async_remote_copy(
            src_ref=block(z * both + (1 - core) * own, own),
            dst_ref=relayed.at[l, :, columns(z)],
            send_sem=s2,
            recv_sem=r2,
            device_id=(me, c + 1 - 2 * core),
            device_id_type=MESH,
        ).start()
        pltpu.make_async_copy(block(c * own, own), relayed.at[l, :, columns(z)], local_sem.at[3]).start()

    def forward(ls, late):
        for m in range(chips - 2, 0, -1):
            for l in ls:
                for e in range(1, chips - m):
                    for up in (1, -1):
                        s, t = z - up * e, z + up * m
                        crossed = (s < half) != (z < half)
                        held = (s >= 0) & (s < chips) & (t >= 0) & (t < chips)

                        @pl.when(held & (crossed if late else jnp.logical_not(crossed)))
                        def _():
                            here, arrived = waiting(z, l, s, t)
                            pltpu.make_async_copy(here, here, arrived).wait()
                            hop(l, s, m, up, lambda at, length: here.at[pl.ds(pl.multiple_of(at, own), length)], s3)

    far = [k for k in range(1, rows) if k not in near]
    every = [0] + near + far
    from_row(near)
    from_above(1, [0] + near)
    from_below(1, [0] + near)
    from_row(far)

    @pl.loop(1, layers)
    def _(l):
        for k in range(1, rows):
            row_copy(l, partner(k)).start()

    from_above(1, far)
    own_mid.wait()
    layer_step(1)
    from_below(1, far)
    for step in range(2, chips):
        from_above(step, every)
        if step < layers:
            layer_step(step)
        if step <= layers:
            forward([step - 1], False)
        from_below(step, every)

    events = [[] for _ in range(KVH + 1)]

    def plan(slot, *event):
        events[min(slot, KVH)].append(event)

    following = max(chips, 2)
    for l in range(following, layers):
        plan(l - following, layer_step, l)
    first = max(chips - 1, 1)
    for l in range(first, layers - 2):
        plan(l - first, forward, [l], False)
    last = [l for l in range(layers - 2, layers) if l >= first]
    if last:
        plan(layers - 1 - first, forward, last, False)
    for l in range(1, layers):
        plan(l + 1, forward, [l], True)

    def run(slot):
        for act, *rest in events[slot]:
            act(*rest)

    @pl.loop(0, seen(z))
    def _(j):
        at = j * rows + me
        key = lax.broadcasted_iota(jnp.int32, (own, slots), 1)
        query = lax.broadcasted_iota(jnp.int32, (own, slots), 0)
        section = key // SUMLEN
        reach = jnp.zeros((own, slots), jnp.int32)
        for s in range(SECTIONS):
            reach = jnp.where((section == s) & (s < counts[at]), BLOCK * blocks[s, at], reach)
        allowed = (key - section * SUMLEN < reach) & (j * slots + key <= c * own + query)
        bias[j] = jnp.where(allowed, 0.0, NEGATIVE)

    for other in range(chips):
        slice_index = 2 * other + 1 - core

        @pl.loop(0, seen(z))
        def _(j):
            kv_doc(slice_index, j, side_sem, c).wait_recv()

    q_copy.wait()
    for t in range(ctx):
        pltpu.make_async_copy(
            kv.at[t, pl.ds(pl.multiple_of(c * own, own), own)],
            relayed.at[0, :, pl.ds(t * feat, feat)],
            local_sem.at[4],
        ).start()

    factor = math.log2(math.e) / math.sqrt(HD)

    @pl.loop(0, KVH)
    def _(k):
        for slot in range(KVH):
            if events[slot]:

                @pl.when(k == slot)
                def _():
                    run(slot)

        per = feat // HD
        key_slice = k // per
        value_slice = (KVH + k) // per
        lanes = pl.ds(pl.multiple_of((k % per) * HD, HD), HD)
        for i in range(GROUP):
            column = pl.ds(pl.multiple_of((k * GROUP + i) * HD, HD), HD)
            q = q_vmem[:, column]

            def block(j, state):
                top, total, acc = state
                at = pl.ds(pl.multiple_of(j * slots, slots), slots)
                s = lax.dot_general(
                    q, kv[key_slice, at, lanes], (((1,), (1,)), ((), ())), preferred_element_type=jnp.float32
                )
                s = s + bias[j]
                newest = jnp.maximum(top, jnp.max(s, axis=1, keepdims=True))
                w = jnp.exp2((s - newest) * factor)
                shrink = jnp.exp2((top - newest) * factor)
                total = total * shrink + jnp.sum(w, axis=1, keepdims=True)
                acc = acc * shrink + jnp.dot(
                    w.astype(jnp.bfloat16), kv[value_slice, at, lanes], preferred_element_type=jnp.float32
                )
                return newest, total, acc

            start = (
                jnp.full((own, 1), NEGATIVE, jnp.float32),
                jnp.zeros((own, 1), jnp.float32),
                jnp.zeros((own, HD), jnp.float32),
            )
            _, total, acc = lax.fori_loop(0, seen(z), block, start)
            out_vmem[:, column] = (acc / total).astype(jnp.bfloat16)

    out_copy = pltpu.make_async_copy(out_vmem, attended, local_sem.at[1])
    out_copy.start()
    run(KVH)

    @pl.loop(0, ctx)
    def _(t):
        @pl.loop(0, rows)
        def _(j):
            @pl.when(t % 2 == core)
            def _():
                chip = t // 2

                @pl.when((z < chips - 1) & (chip <= z))
                def _():
                    kv_doc(t, j, up_sem, c).wait_send()

                @pl.when((z > 0) & (j < seen(z - 1)) & (chip >= z))
                def _():
                    kv_doc(t, j, down_sem, c).wait_send()

                @pl.when(j < seen(z))
                def _():
                    kv_doc(t, j, side_sem, c).wait_send()

    def sized(ref, sem):
        return pltpu.make_async_copy(ref, ref, sem)

    sized(cache.at[:, pl.ds(0, rows - 1)], s1).wait()
    passed = relayed.at[pl.ds(1, layers - 1), :, pl.ds(0, (ctx - 1) * feat)]
    sized(passed, s2).wait()
    for q in range(chips):
        kept = 2 * q * (chips - 1 - q)
        if kept:

            @pl.when(z == q)
            def _():
                sized(fwd.at[:, pl.ds(0, kept)], s3).wait()

    sized(passed, r2).wait()
    sized(relayed.at[pl.ds(1, layers - 1), :, pl.ds(0, feat)], local_sem.at[3]).wait()
    sized(relayed.at[0], local_sem.at[4]).wait()
    out_copy.wait()


def copy_out(attended, relayed, attended_out, relayed_out, sems):
    layers = relayed.shape[0]
    copies = [pltpu.make_async_copy(relayed.at[l], relayed_out.at[l], sems.at[l]) for l in range(layers)]
    copies.append(pltpu.make_async_copy(attended, attended_out, sems.at[layers]))
    for copy in copies:
        copy.start()
    for copy in copies:
        copy.wait()


def deliver(attended, relayed):
    any_space = pl.BlockSpec(memory_space=pl.ANY)
    return pl.pallas_call(
        copy_out,
        out_shape=(
            jax.ShapeDtypeStruct(attended.shape, attended.dtype),
            jax.ShapeDtypeStruct(relayed.shape, relayed.dtype),
        ),
        in_specs=[any_space, any_space],
        out_specs=(any_space, any_space),
        scratch_shapes=[pltpu.SemaphoreType.DMA((relayed.shape[0] + 1,))],
        compiler_params=pltpu.CompilerParams(vmem_limit_bytes=4 * 1024 * 1024),
    )(attended, relayed)


def local(summary_cache, queries, section_counts, summary_blocks):
    rows = lax.axis_size("doc")
    ctx = lax.axis_size("ctx")
    layers, documents, slots, feat = summary_cache.shape
    own = queries.shape[1]
    dtype = summary_cache.dtype
    any_space = pl.BlockSpec(memory_space=pl.ANY)
    in_place = pl.BlockSpec(memory_space=pltpu.HBM)
    scalars = pl.BlockSpec(memory_space=pltpu.SMEM)
    dma = pltpu.SemaphoreType.DMA
    size = rows * slots * feat * (ctx + layers) * 2 + own * queries.shape[2] * 4 + rows * own * slots * 4
    edge = (ctx // 2 - 1) // 2
    held = max(2 * edge * (ctx // 2 - 1 - edge), 1)
    size = size + (layers - 1) * held * 4 * own * feat
    room = size + own * (layers * ctx * feat + queries.shape[2]) * 2 + 4 * 1024 * 1024
    place = pltpu.VMEM if room < 60 * 1024 * 1024 else pltpu.HBM

    def in_hbm(array):
        return pltpu.with_memory_space_constraint(array, pltpu.HBM)

    attended, relayed = pl.pallas_call(
        functools.partial(kernel, rows, ctx),
        out_shape=(
            place(queries.shape[1:], dtype),
            place((layers, own, ctx * feat), dtype),
        ),
        in_specs=[in_place, in_place, scalars, scalars],
        out_specs=(any_space, any_space),
        scratch_shapes=[
            pltpu.VMEM((ctx, rows * slots, feat), dtype),
            pltpu.VMEM((layers - 1, rows * slots, feat), dtype),
            pltpu.VMEM((rows - 1, slots, feat), dtype),
            pltpu.VMEM((layers - 1, held, 2 * own, feat), dtype),
            pltpu.VMEM(queries.shape[1:], dtype),
            pltpu.VMEM(queries.shape[1:], dtype),
            pltpu.VMEM((rows, own, slots), jnp.float32),
            dma,
            dma((rows, PARTS)),
            dma((layers,)),
            dma((ctx // 2, rows)),
            dma((ctx // 2, rows)),
            dma((ctx // 2, rows)),
            dma((ctx, rows, PARTS)),
            dma,
            dma,
            dma((5,)),
            dma((rows - 1,)),
            pltpu.SemaphoreType.REGULAR((rows,)),
            dma((layers - 1, held)),
            dma,
        ],
        compiler_params=pltpu.CompilerParams(
            collective_id=0, has_side_effects=True, vmem_limit_bytes=size + 3 * 1024 * 1024
        ),
    )(*(in_hbm(x) for x in (summary_cache, queries[0], section_counts, summary_blocks.T)))
    return deliver(attended[None], relayed[:, None])


def solution(mesh):
    placed = (P(None, "doc", None, "ctx"), P("doc", "ctx", None), P(), P())
    return jax.shard_map(
        local,
        mesh=mesh,
        in_specs=placed,
        out_specs=(P("doc", "ctx", None), P(None, "doc", "ctx", None)),
        check_vma=False,
    )
```

profile of v0, /device:TPU:29, one launch (start us, length us, event | category | flops | bytes accessed | tf_op | source)
XLA Modules:
  0.0 214.3 jit_solution(12734487598879031269)
XLA Ops:
  0.6 209.6 %shard_map.59 = (bf16[256,4096]{1,0:T(8,128)(2,1)S(1)}, bf16[8,256,2048]{2,1,0:T(8,128)(2,1)S(1)}) custom-call(bf16[8,4,512,256]{3,2,1,0:T(8,128)(2,1)} %cache.1, bf16[256,4096]{1,0:T(8,128)(2,1)} %bitcast.6, s32[16]{0:T(128)} %counts.1, s32[2,16]{1,0:T(2,128)} %bitcast.7), custom_call_target="tpu_custom_call" | custom-call | tf_op jit(solution)/shard_map/pallas_call | solution.py:515
  210.2 4.0 %shard_map.60 = (bf16[1,256,4096]{2,1,0:T(8,128)(2,1)}, bf16[8,1,256,2048]{3,2,1,0:T(8,128)(2,1)}) custom-call(bf16[1,256,4096]{2,1,0:T(8,128)(2,1)S(1)} %bitcast.5, bf16[8,1,256,2048]{3,2,1,0:T(8,128)(2,1)S(1)} %bitcast.4), custom_call_target="tpu_custom_call" | custom-call | tf_op jit(solution)/shard_map/pallas_call | solution.py:482
where the time goes:
time: 215 us; the launch traced here: 214 us
  Pallas kernels  214 us (100%)
    pallas_call x1, Pallas kernels, local(): pl.pallas_call(functools.partial(kernel, rows, ctx), out_shape=(place(que...  210 us

commit v1 on v0

--- a/solution.py
+++ b/solution.py
@@ -15,7 +15,7 @@
 SECTIONS = 2
 GROUP = 4
 SUMLEN = 256
-PARTS = 4
+PARTS = 2
 
 
 NEGATIVE = -1e30
@@ -46,7 +46,9 @@
     up_sem,
     down_sem,
     side_sem,
-    kv_sem,
+    across_sem,
+    part_sem,
+    doc_sem,
     s2,
     r2,
     local_sem,
@@ -58,7 +60,7 @@
     layers, _, slots, feat = cache.shape
     own = queries.shape[0]
     chips = ctx // 2
-    parts = kv_sem.shape[2]
+    parts = part_sem.shape[2]
     size = slots // parts
     me = lax.axis_index("doc")
     c = lax.axis_index("ctx")
@@ -145,51 +147,62 @@
             device_id_type=MESH,
         )
 
-    def kv_part(slice_index, j, h, sems, target):
+    def kv_copy(slice_index, j, h, sent, arrived, target):
+        ref = doc(slice_index, j) if h is None else part(slice_index, j, h)
         return pltpu.make_async_remote_copy(
-            src_ref=part(slice_index, j, h),
-            dst_ref=part(slice_index, j, h),
-            send_sem=sems.at[slice_index // 2, j],
-            recv_sem=kv_sem.at[slice_index, j, h],
+            src_ref=ref,
+            dst_ref=ref,
+            send_sem=sent,
+            recv_sem=arrived,
             device_id=(me, target),
             device_id_type=MESH,
         )
 
-    def kv_doc(slice_index, j, sems, target):
-        return pltpu.make_async_remote_copy(
-            src_ref=doc(slice_index, j),
-            dst_ref=doc(slice_index, j),
-            send_sem=sems.at[slice_index // 2, j],
-            recv_sem=kv_sem.at[slice_index, j, 0],
-            device_id=(me, target),
-            device_id_type=MESH,
-        )
-
-    def pass_up(slice_index, j, h):
-        @pl.when(z < chips - 1)
-        def _():
-            kv_part(slice_index, j, h, up_sem, c + 2).start()
-
-    def pass_down(slice_index, j, h):
-        @pl.when((z > 0) & (j < seen(z - 1)))
-        def _():
-            kv_part(slice_index, j, h, down_sem, c - 2).start()
+    early = [0] + near
+
+    def arrival(way, step, k, h):
+        if step == 1 and k in early:
+            return part_sem.at[way, early.index(k), 0 if h is None else h]
+        return doc_sem.at[way, step - 1, k]
+
+    def up_copy(step, k, h):
+        return kv_copy(c - 2 * step, partner(k), h, up_sem, arrival(0, step + 1, k, h), c + 2)
+
+    def down_copy(step, k, h):
+        return kv_copy(c + 2 * step, partner(k), h, down_sem, arrival(1, step + 1, k, h), c - 2)
+
+    def pass_up(step, k, h):
+        if step + 1 < chips:
+
+            @pl.when(z < chips - 1)
+            def _():
+                up_copy(step, k, h).start()
+
+    def pass_down(step, k, h):
+        if step + 1 < chips:
+
+            @pl.when((z > 0) & (partner(k) < seen(z - 1)))
+            def _():
+                down_copy(step, k, h).start()
+
+    def side_copy(slice_index, j):
+        return kv_copy(slice_index, j, None, side_sem, across_sem, c + 1 - 2 * core)
 
     def pass_side(slice_index, j):
         @pl.when(j < seen(z))
         def _():
-            kv_doc(slice_index, j, side_sem, c + 1 - 2 * core).start()
+            side_copy(slice_index, j).start()
 
     own_kv.wait()
     for h in range(parts):
-        pass_up(c, me, h)
+        pass_up(0, 0, h)
     for k in near:
         staged(k).wait()
     for h in range(parts):
         for k in near:
             first_copy(k, partner(k), me, h).start()
     for h in range(parts):
-        pass_down(c, me, h)
+        pass_down(0, 0, h)
     pass_side(c, me)
     own_mid.start()
     q_copy.start()
@@ -208,33 +221,34 @@
             for k in ks:
                 j = partner(k)
                 first_copy(k, me, j, h).wait_recv()
-                pass_up(c, j, h)
-                pass_down(c, j, h)
+                pass_up(0, k, h)
+                pass_down(0, k, h)
                 if h == parts - 1:
                     pass_side(c, j)
+
+    def pieces_of(step, k):
+        return range(parts) if step == 1 and k in early else [None]
 
     def from_below(step, ks):
         @pl.when(z >= step)
         def _():
             for k in ks:
-                j = partner(k)
-                for h in range(parts):
-                    kv_part(c - 2 * step, j, h, up_sem, c).wait_recv()
-                    pass_up(c - 2 * step, j, h)
-                pass_side(c - 2 * step, j)
+                for h in pieces_of(step, k):
+                    kv_copy(c - 2 * step, partner(k), h, up_sem, arrival(0, step, k, h), c).wait_recv()
+                    pass_up(step, k, h)
+                pass_side(c - 2 * step, partner(k))
 
     def from_above(step, ks):
         @pl.when(z + step < chips)
         def _():
             for k in ks:
-                j = partner(k)
-
-                @pl.when(j < seen(z))
+
+                @pl.when(partner(k) < seen(z))
                 def _():
-                    for h in range(parts):
-                        kv_part(c + 2 * step, j, h, down_sem, c).wait_recv()
-                        pass_down(c + 2 * step, j, h)
-                    pass_side(c + 2 * step, j)
+                    for h in pieces_of(step, k):
+                        kv_copy(c + 2 * step, partner(k), h, down_sem, arrival(1, step, k, h), c).wait_recv()
+                        pass_down(step, k, h)
+                    pass_side(c + 2 * step, partner(k))
 
     both = 2 * own
     half = chips // 2
@@ -293,10 +307,12 @@
         ).start()
         pltpu.make_async_copy(block(c * own, own), relayed.at[l, :, columns(z)], local_sem.at[3]).start()
 
-    def forward(ls, late):
+    def forward(ls, hops, late):
         for m in range(chips - 2, 0, -1):
             for l in ls:
-                for e in range(1, chips - m):
+                for e in hops:
+                    if e + m > chips - 1:
+                        continue
                     for up in (1, -1):
                         s, t = z - up * e, z + up * m
                         crossed = (s < half) != (z < half)
@@ -309,10 +325,11 @@
                             hop(l, s, m, up, lambda at, length: here.at[pl.ds(pl.multiple_of(at, own), length)], s3)
 
     far = [k for k in range(1, rows) if k not in near]
-    every = [0] + near + far
+    every = early + far
+    hops = range(1, chips - 1)
     from_row(near)
-    from_above(1, [0] + near)
-    from_below(1, [0] + near)
+    from_above(1, early)
+    from_below(1, early)
     from_row(far)
 
     @pl.loop(1, layers)
@@ -329,7 +346,7 @@
         if step < layers:
             layer_step(step)
         if step <= layers:
-            forward([step - 1], False)
+            forward([step - 1], hops, False)
         from_below(step, every)
 
     events = [[] for _ in range(KVH + 1)]
@@ -338,16 +355,21 @@
         events[min(slot, KVH)].append(event)
 
     following = max(chips, 2)
+    first = max(chips - 1, 1)
+    last = [l for l in range(layers - 2, layers) if l >= first]
+    late = sorted((l + 2 * e, -e) for l in range(1, layers) for e in hops)
     for l in range(following, layers):
         plan(l - following, layer_step, l)
-    first = max(chips - 1, 1)
+    for total, e in late:
+        if e < -1:
+            plan(max(0, (total - 4) * 4 // 3), forward, [total + 2 * e], [-e], True)
     for l in range(first, layers - 2):
-        plan(l - first, forward, [l], False)
-    last = [l for l in range(layers - 2, layers) if l >= first]
+        plan(l - first + 1, forward, [l], hops, False)
     if last:
-        plan(layers - 1 - first, forward, last, False)
-    for l in range(1, layers):
-        plan(l + 1, forward, [l], True)
+        plan(layers - 2, forward, last, hops, False)
+    for total, e in late:
+        if e == -1:
+            plan(max(0, (total - 4) * 4 // 3), forward, [total - 2], [1], True)
 
     def run(slot):
         for act, *rest in events[slot]:
@@ -365,12 +387,14 @@
         allowed = (key - section * SUMLEN < reach) & (j * slots + key <= c * own + query)
         bias[j] = jnp.where(allowed, 0.0, NEGATIVE)
 
-    for other in range(chips):
-        slice_index = 2 * other + 1 - core
-
-        @pl.loop(0, seen(z))
-        def _(j):
-            kv_doc(slice_index, j, side_sem, c).wait_recv()
+    def sized(ref, sem):
+        return pltpu.make_async_copy(ref, ref, sem)
+
+    for q in range(chips):
+
+        @pl.when(z == q)
+        def _():
+            sized(kv.at[pl.ds(0, chips), pl.ds(0, seen(q) * slots)], across_sem).wait()
 
     q_copy.wait()
     for t in range(ctx):
@@ -427,28 +451,15 @@
     out_copy.start()
     run(KVH)
 
-    @pl.loop(0, ctx)
-    def _(t):
-        @pl.loop(0, rows)
-        def _(j):
-            @pl.when(t % 2 == core)
-            def _():
-                chip = t // 2
-
-                @pl.when((z < chips - 1) & (chip <= z))
-                def _():
-                    kv_doc(t, j, up_sem, c).wait_send()
-
-                @pl.when((z > 0) & (j < seen(z - 1)) & (chip >= z))
-                def _():
-                    kv_doc(t, j, down_sem, c).wait_send()
-
-                @pl.when(j < seen(z))
-                def _():
-                    kv_doc(t, j, side_sem, c).wait_send()
-
-    def sized(ref, sem):
-        return pltpu.make_async_copy(ref, ref, sem)
+    for q in range(chips):
+
+        @pl.when(z == q)
+        def _():
+            if q < chips - 1:
+                sized(kv.at[pl.ds(0, q + 1)], up_sem).wait()
+            if q > 0:
+                sized(kv.at[pl.ds(0, chips - q), pl.ds(0, seen(q - 1) * slots)], down_sem).wait()
+            sized(kv.at[pl.ds(0, chips), pl.ds(0, seen(q) * slots)], side_sem).wait()
 
     sized(cache.at[:, pl.ds(0, rows - 1)], s1).wait()
     passed = relayed.at[pl.ds(1, layers - 1), :, pl.ds(0, (ctx - 1) * feat)]
@@ -531,15 +542,17 @@
             dma,
             dma((rows, PARTS)),
             dma((layers,)),
-            dma((ctx // 2, rows)),
-            dma((ctx // 2, rows)),
-            dma((ctx // 2, rows)),
-            dma((ctx, rows, PARTS)),
+            dma,
+            dma,
+            dma,
+            dma,
+            dma((2, rows, PARTS)),
+            dma((2, max(ctx // 2 - 1, 1), rows)),
             dma,
             dma,
             dma((5,)),
             dma((rows - 1,)),
-            pltpu.SemaphoreType.REGULAR((rows,)),
+            pltpu.SemaphoreType.REGULAR((max(rows.bit_length() - 2, 1),)),
             dma((layers - 1, held)),
             dma,
         ],

time: 215 us -> 212 us (0.986); the launches traced: 214 us -> 208 us
  Pallas kernels: 214 us -> 207 us
    pallas_call x1, Pallas kernels: 210 us -> 203 us  [local(): pl.pallas_call(functools.partial(kernel, rows, ctx), out_shape=(place(que...]
where the time goes in v1:
time: 212 us; the launch traced here: 208 us
  Pallas kernels  207 us (98%)
    pallas_call x1, Pallas kernels, local(): pl.pallas_call(functools.partial(kernel, rows, ctx), out_shape=(place(que...  203 us

profile of v1, /device:TPU:29, one launch (start us, length us, event | category | flops | bytes accessed | tf_op | source)
XLA Modules:
  0.0 207.6 jit_solution(1334938801377606401)
XLA Ops:
  0.6 202.9 %shard_map.59 = (bf16[256,4096]{1,0:T(8,128)(2,1)S(1)}, bf16[8,256,2048]{2,1,0:T(8,128)(2,1)S(1)}) custom-call(bf16[8,4,512,256]{3,2,1,0:T(8,128)(2,1)} %cache.1, bf16[256,4096]{1,0:T(8,128)(2,1)} %bitcast.6, s32[16]{0:T(128)} %counts.1, s32[2,16]{1,0:T(2,128)} %bitcast.7), custom_call_target="tpu_custom_call" | custom-call | tf_op jit(solution)/shard_map/pallas_call | solution.py:526
  203.6 4.0 %shard_map.60 = (bf16[1,256,4096]{2,1,0:T(8,128)(2,1)}, bf16[8,1,256,2048]{3,2,1,0:T(8,128)(2,1)}) custom-call(bf16[1,256,4096]{2,1,0:T(8,128)(2,1)S(1)} %bitcast.5, bf16[8,1,256,2048]{3,2,1,0:T(8,128)(2,1)S(1)} %bitcast.4), custom_call_target="tpu_custom_call" | custom-call | tf_op jit(solution)/shard_map/pallas_call | solution.py:493

commit v2 on v1

--- a/solution.py
+++ b/solution.py
@@ -29,8 +29,8 @@
     ctx,
     cache,
     queries,
-    counts,
-    blocks,
+    counts_in,
+    blocks_in,
     attended,
     relayed,
     kv,
@@ -56,6 +56,9 @@
     hello,
     fwd_sem,
     s3,
+    counts,
+    blocks,
+    table_sem,
 ):
     layers, _, slots, feat = cache.shape
     own = queries.shape[0]
@@ -119,6 +122,12 @@
         mid.at[:, pl.ds(pl.multiple_of(me * slots, slots), slots)],
         local_sem.at[2],
     )
+    tables = [
+        pltpu.make_async_copy(counts_in, counts, table_sem.at[0]),
+        pltpu.make_async_copy(blocks_in, blocks, table_sem.at[1]),
+    ]
+    for copy in tables:
+        copy.start()
     pl.semaphore_wait(barrier, 2 * sides + len(near) + 1)
 
     def doc(slice_index, j):
@@ -375,6 +384,9 @@
         for act, *rest in events[slot]:
             act(*rest)
 
+    for copy in tables:
+        copy.wait()
+
     @pl.loop(0, seen(z))
     def _(j):
         at = j * rows + me
@@ -479,13 +491,15 @@
 
 
 def copy_out(attended, relayed, attended_out, relayed_out, sems):
-    layers = relayed.shape[0]
-    copies = [pltpu.make_async_copy(relayed.at[l], relayed_out.at[l], sems.at[l]) for l in range(layers)]
-    copies.append(pltpu.make_async_copy(attended, attended_out, sems.at[layers]))
-    for copy in copies:
-        copy.start()
-    for copy in copies:
-        copy.wait()
+    for l in range(relayed.shape[0]):
+        for h in range(2):
+            rows = pl.ds(h * relayed.shape[2] // 2, relayed.shape[2] // 2)
+            pltpu.make_async_copy(relayed.at[l, :, rows], relayed_out.at[l, :, rows], sems.at[1]).start()
+    for h in range(4):
+        rows = pl.ds(h * attended.shape[1] // 4, attended.shape[1] // 4)
+        pltpu.make_async_copy(attended.at[:, rows], attended_out.at[:, rows], sems.at[0]).start()
+    pltpu.make_async_copy(attended, attended_out, sems.at[0]).wait()
+    pltpu.make_async_copy(relayed, relayed_out, sems.at[1]).wait()
 
 
 def deliver(attended, relayed):
@@ -498,7 +512,7 @@
         ),
         in_specs=[any_space, any_space],
         out_specs=(any_space, any_space),
-        scratch_shapes=[pltpu.SemaphoreType.DMA((relayed.shape[0] + 1,))],
+        scratch_shapes=[pltpu.SemaphoreType.DMA((2,))],
         compiler_params=pltpu.CompilerParams(vmem_limit_bytes=4 * 1024 * 1024),
     )(attended, relayed)
 
@@ -511,7 +525,6 @@
     dtype = summary_cache.dtype
     any_space = pl.BlockSpec(memory_space=pl.ANY)
     in_place = pl.BlockSpec(memory_space=pltpu.HBM)
-    scalars = pl.BlockSpec(memory_space=pltpu.SMEM)
     dma = pltpu.SemaphoreType.DMA
     size = rows * slots * feat * (ctx + layers) * 2 + own * queries.shape[2] * 4 + rows * own * slots * 4
     edge = (ctx // 2 - 1) // 2
@@ -529,7 +542,7 @@
             place(queries.shape[1:], dtype),
             place((layers, own, ctx * feat), dtype),
         ),
-        in_specs=[in_place, in_place, scalars, scalars],
+        in_specs=[in_place] * 4,
         out_specs=(any_space, any_space),
         scratch_shapes=[
             pltpu.VMEM((ctx, rows * slots, feat), dtype),
@@ -555,6 +568,9 @@
             pltpu.SemaphoreType.REGULAR((max(rows.bit_length() - 2, 1),)),
             dma((layers - 1, held)),
             dma,
+            pltpu.SMEM(section_counts.shape, jnp.int32),
+            pltpu.SMEM(summary_blocks.shape[::-1], jnp.int32),
+            dma((2,)),
         ],
         compiler_params=pltpu.CompilerParams(
             collective_id=0, has_side_effects=True, vmem_limit_bytes=size + 3 * 1024 * 1024

time: 212 us -> 211 us (level)
  no operation moved by 1% of the time
where the time goes in v2:
time: 211 us; the launch traced here: 207 us
  Pallas kernels  206 us (98%)
    pallas_call x1, Pallas kernels, local(): pl.pallas_call(functools.partial(kernel, rows, ctx), out_shape=(place(que...  202 us

profile of v2, /device:TPU:29, one launch (start us, length us, event | category | flops | bytes accessed | tf_op | source)
XLA Modules:
  0.0 206.8 jit_solution(8103166897091380167)
XLA Ops:
  0.6 202.2 %shard_map.59 = (bf16[256,4096]{1,0:T(8,128)(2,1)S(1)}, bf16[8,256,2048]{2,1,0:T(8,128)(2,1)S(1)}) custom-call(bf16[8,4,512,256]{3,2,1,0:T(8,128)(2,1)} %cache.1, bf16[256,4096]{1,0:T(8,128)(2,1)} %bitcast.6, s32[16]{0:T(128)} %counts_in.1, s32[2,16]{1,0:T(2,128)} %bitcast.7), custom_call_target="tpu_custom_call" | custom-call | tf_op jit(solution)/shard_map/pallas_call | solution.py:539
  202.9 3.9 %shard_map.60 = (bf16[1,256,4096]{2,1,0:T(8,128)(2,1)}, bf16[8,1,256,2048]{3,2,1,0:T(8,128)(2,1)}) custom-call(bf16[1,256,4096]{2,1,0:T(8,128)(2,1)S(1)} %bitcast.5, bf16[8,1,256,2048]{3,2,1,0:T(8,128)(2,1)S(1)} %bitcast.4), custom_call_target="tpu_custom_call" | custom-call | tf_op jit(solution)/shard_map/pallas_call | solution.py:507
